TPU v7x, 256 devices: a whole 4x4x8 slice. The times are simulated.
256 devices in a mesh: rows: 64 (over z, y, core), cols: 4 (over x).
Axes of the slice: x: 4, y: 4, z: 8, core: 2. Of those that a mesh axis runs over, the one named last changes fastest.
Arguments:
- gradients: float32 [256, 128, 4096], P(None, 'rows', 'cols'), may hold values from -6 to 6
- momentum: float32 [256, 128, 4096], P(None, 'rows', 'cols'), may hold values from -6 to 6
- weights: float32 [256, 128, 4096], P(None, 'rows', 'cols'), may hold values from -0.1875 to 0.1875
Outputs:
- new_weights: float32 [256, 128, 4096], P(None, 'rows', 'cols')
- new_momentum: float32 [256, 128, 4096], P(None, 'rows', 'cols')
All inputs are finite; a program needn't handle non-finite values.
Results may differ from a plain program's by a relative error of at most 0.0003.
Values sent between devices are 32-bit elements.
A program may use at most 64 MiB of HBM per device.

v0:
```python
import jax
import jax.numpy as jnp
from jax import lax
from jax.sharding import PartitionSpec as P

ITERS = 4


hold_rate = 0.8
learn_rate = 0.8
decay_rate = 0.1


def local(gradients, momentum, weights):
    new_momentum = hold_rate * momentum + gradients
    moved = lax.all_to_all(new_momentum, "rows", split_axis=0, concat_axis=1, tiled=True)
    whole = lax.all_to_all(moved, "cols", split_axis=0, concat_axis=2, tiled=True)
    iterate = whole * lax.rsqrt(jnp.sum(whole * whole, axis=(1, 2), keepdims=True) + 1e-06)
    for step in range(ITERS):
        gram = jnp.einsum("mik,mjk->mij", iterate, iterate, precision=lax.Precision.HIGHEST)
        mixed = -4.775 * gram + 2.0315 * jnp.einsum(
            "mij,mjk->mik", gram, gram, precision=lax.Precision.HIGHEST
        )
        iterate = 3.4445 * iterate + jnp.einsum(
            "mij,mjk->mik", mixed, iterate, precision=lax.Precision.HIGHEST
        )
    iterate = lax.all_to_all(iterate, "cols", split_axis=2, concat_axis=0, tiled=True)
    back = lax.all_to_all(iterate, "rows", split_axis=1, concat_axis=0, tiled=True)
    new_weights = (1.0 - learn_rate * decay_rate) * weights - learn_rate * back
    return (new_weights, new_momentum)


def solution(mesh):
    placed = (P(None, "rows", "cols"), P(None, "rows", "cols"), P(None, "rows", "cols"))
    return jax.shard_map(
        local,
        mesh=mesh,
        in_specs=placed,
        out_specs=(P(None, "rows", "cols"), P(None, "rows", "cols")),
        check_vma=False,
    )
```

profile of v0, /device:TPU:1, one launch (start us, length us, event | category | flops | bytes accessed | tf_op | source)
XLA Modules:
  0.0 228.9 jit_solution(2761105436010172675)
XLA Ops:
  0.6 3.7 %multiply_add_fusion = f32[256,2,1024]{2,1,0:T(2,128)S(1)} fusion(f32[256,2,1024]{2,1,0:T(2,128)} %param.3, f32[256,2,1024]{2,1,0:T(2,128)} %param.4), kind=kLoop, calls=%fused_computation.11 | loop fusion | flops 1048576 | bytes 6291456 | tf_op jit(solution)/shard_map/add | solution.py:15
  4.3 63.3 %all_to_all.54 = f32[256,2,1024]{2,1,0:T(2,128)S(1)} all-to-all(f32[256,2,1024]{2,1,0:T(2,128)S(1)} %multiply_add_fusion), channel_id=1, replica_groups=mesh['rows'=64,'cols'=4] {'rows'}, dimensions={0} | all-to-all | bytes 4194304 | tf_op jit(solution)/shard_map/all_to_all | solution.py:16
  67.6 0.8 copy.32
  68.4 2.4 %all_to_all.43 = f32[4,128,1024]{2,1,0:T(8,128)} reshape(f32[4,64,2,1024]{3,2,1,0:T(2,128)S(1)} %bitcast.56) | data formatting | bytes 4194304 | tf_op jit(solution)/shard_map/all_to_all | solution.py:16
  70.8 28.7 %all_to_all.55 = f32[4,128,1024]{2,1,0:T(8,128)S(1)} all-to-all(f32[4,128,1024]{2,1,0:T(8,128)} %all_to_all.43), channel_id=1, replica_groups=mesh['rows'=64,'cols'=4] {'cols'}, dimensions={0} | all-to-all | bytes 4194304 | tf_op jit(solution)/shard_map/all_to_all | solution.py:17
  99.5 1.1 multiply_reduce_fusion
  101.4 1.8 fusion.4
  103.4 2.6 %multiply_bitcast_fusion.1 = (f32[1,128,4,1024]{3,1,2,0:T(8,128)}, f32[1,128,4,1024]{3,1,2,0:T(8,128)}) fusion(f32[4,128,1024]{2,1,0:T(8,128)S(1)} %all_to_all.55, f32[]{:T(128)S(6)} %rsqrt.4), kind=kLoop, calls=%fused_computation.13 | loop fusion | flops 1048576 | bytes 6291460 | tf_op jit(solution)/shard_map/mul | solution.py:18
  105.9 1.9 copy.26
  107.8 2.9 %copy.25 = f32[1,128,4,1024]{1,3,2,0:T(8,128)} copy(f32[1,128,4,1024]{3,1,2,0:T(8,128)} %get-tuple-element.3) | data formatting | bytes 4194304 | tf_op jit(solution)/shard_map/mul | solution.py:24
  110.7 3.0 %copy.27 = f32[128,4096]{1,0:T(8,128)} copy(f32[128,4096]{0,1:T(8,128)} %bitcast.57) | data formatting | bytes 4194304 | tf_op jit(solution)/shard_map/mul | solution.py:24
  113.7 3.6 %convolution_add_fusion.3 = f32[128,4096]{1,0:T(8,128)S(1)} fusion(f32[128,4096]{1,0:T(8,128)} %copy.27, f32[128,128]{1,0:T(8,128)S(1)} %fusion.10, f32[128,4096]{0,1:T(8,128)S(1)} %bitcast.55), kind=kOutput, calls=%fused_computation.4 | convolution fusion | flops 805830656 | bytes 6356992 | tf_op jit(solution)/shard_map/mij,mjk->mik/dot_general | solution.py:24
  117.3 1.8 fusion.12
  119.3 2.0 convolution_add_fusion.2
  121.3 1.8 fusion.13
  123.3 2.0 convolution_add_fusion.1
  125.4 1.8 fusion.14
  127.4 2.3 fusion
  129.7 3.7 %copy.28 = f32[1,128,4096]{1,0,2:T(1,128)} copy(f32[1,128,4096]{2,1,0:T(8,128)S(1)} %fusion) | data formatting | bytes 4194304 | tf_op jit(solution)/shard_map/add | solution.py:24
  133.4 27.0 %all_to_all.56 = f32[1,128,4096]{1,0,2:T(1,128)S(1)} all-to-all(f32[1,128,4096]{1,0,2:T(1,128)} %copy.28), channel_id=1, replica_groups=mesh['rows'=64,'cols'=4] {'cols'}, dimensions={2} | all-to-all | bytes 4194304 | tf_op jit(solution)/shard_map/all_to_all | solution.py:27
  160.4 2.0 copy.29
  162.3 61.1 %all_to_all.57 = f32[4,128,1024]{2,0,1:T(4,128)S(1)} all-to-all(f32[4,128,1024]{2,0,1:T(4,128)} %bitcast.59), channel_id=1, replica_groups=mesh['rows'=64,'cols'=4] {'rows'}, dimensions={1} | all-to-all | bytes 4194304 | tf_op jit(solution)/shard_map/all_to_all | solution.py:28
  224.0 1.9 copy.30
  226.0 2.9 %bitcast_subtract_fusion = f32[256,2,1024]{2,1,0:T(2,128)} fusion(f32[64,4,2,1024]{3,2,1,0:T(2,128)S(1)} %copy.30, f32[256,2,1024]{2,1,0:T(2,128)S(1)} %copy-done.1), kind=kLoop, calls=%fused_computation.7 | loop fusion | flops 1048576 | bytes 6291456 | tf_op jit(solution)/shard_map/sub | solution.py:29
  (9 shorter events, 1.4 us)
Async XLA Ops:
  4.3 63.3 %copy-start = (f32[256,2,1024]{2,1,0:T(2,128)}, f32[256,2,1024]{2,1,0:T(2,128)S(1)}, u32[]{:S(2)}) copy-start(f32[256,2,1024]{2,1,0:T(2,128)S(1)} %multiply_add_fusion) | copy-start | bytes 6291460
  224.0 2.0 copy-start.1
where the time goes:
time: 230 us; the launch traced here: 229 us
  blocking collectives  180 us (78%)
  local copies, waits for them, and re-layouts  18.6 us (8%)
  matrix products  17.9 us (8%)
  other arithmetic  10.8 us (5%)
    all_to_all x1, blocking collectives, local(): lax.all_to_all(new_momentum, 'rows', split_axis=0, concat_axis=1, tiled=T...  63.3 us
    all_to_all x1, blocking collectives, local(): lax.all_to_all(iterate, 'rows', split_axis=1, concat_axis=0, tiled=True)  61.1 us
    all_to_all x1, blocking collectives, local(): lax.all_to_all(moved, 'cols', split_axis=0, concat_axis=2, tiled=True)  28.7 us
    all_to_all x1, blocking collectives, local(): lax.all_to_all(iterate, 'cols', split_axis=2, concat_axis=0, tiled=True)  27 us
    dot_general x4, matrix products, local(): jnp.einsum('mij,mjk->mik', mixed, iterate, precision=lax.Precision.HIGHEST)  9.94 us
    dot_general x4, matrix products, local(): jnp.einsum('mik,mjk->mij', iterate, iterate, precision=lax.Precision.HIGH...  7.17 us
    mul x2, local copies, waits for them, and re-layouts, local(): 3.4445 * iterate  5.84 us

commit v1 on v0

v1 whole, which is shorter than its diff:
```python
import jax
import jax.numpy as jnp
from jax import lax
from jax.experimental import pallas as pl
from jax.experimental.pallas import tpu as pltpu
from jax.sharding import PartitionSpec as P

ITERS = 4
GROUPS = 4
Z, Y, CORES = 8, 4, 2
ROWS = Z * Y * CORES
COLS = 4
SIDE = 128
LANES = 128
UNIT = 16
WHOLE = ROWS * UNIT
MESH = pl.DeviceIdType.MESH

hold_rate = 0.8
learn_rate = 0.8
decay_rate = 0.1


def product(a, b, over=0):
    return lax.dot_general(
        a, b, (((1,), (over,)), ((), ())),
        precision=lax.Precision.HIGHEST, preferred_element_type=jnp.float32,
    )


def kernel(x_ref, back_ref, held, grams, done, there_send, there_recv, gram_send, gram_recv, back_send, back_recv):
    r = lax.axis_index("rows")
    c = lax.axis_index("cols")
    z, y, k = r // (Y * CORES), (r // CORES) % Y, r % CORES

    def partner(i):
        return (
            lax.rem(z + i % Z, Z) * (Y * CORES)
            + lax.rem(y + (i // Z) % Y, Y) * CORES
            + lax.rem(k + i // (Z * Y), CORES)
        )

    barrier = pltpu.get_barrier_semaphore()

    def greet(i, carry):
        pl.semaphore_signal(barrier, inc=1, device_id=(partner(i), c), device_id_type=MESH)
        return carry

    lax.fori_loop(1, ROWS, greet, 0)
    for step in range(1, COLS):
        pl.semaphore_signal(barrier, inc=1, device_id=(r, lax.rem(c + step, COLS)), device_id_type=MESH)
    pl.semaphore_wait(barrier, ROWS - 1 + COLS - 1)

    def unit(start):
        return pl.ds(pl.multiple_of(start, UNIT), UNIT)

    for g in range(GROUPS):
        def there(i, carry):
            p = partner(i)
            pltpu.make_async_remote_copy(
                x_ref.at[unit((p * GROUPS + g) * UNIT)],
                held.at[unit(g * WHOLE + r * UNIT)],
                there_send, there_recv.at[g],
                device_id=(p, c), device_id_type=MESH,
            ).start()
            return carry

        lax.fori_loop(1, ROWS, there, 0)
    for g in range(GROUPS):
        held[unit(g * WHOLE + r * UNIT), :] = x_ref[unit((r * GROUPS + g) * UNIT), :]

    row = lax.broadcasted_iota(jnp.int32, (SIDE, SIDE), 0)
    col = lax.broadcasted_iota(jnp.int32, (SIDE, SIDE), 1)
    diagonal = row == col
    half = ROWS
    most = pl.ds(0, (ROWS - 1) * UNIT)

    def rows_of(g):
        return jnp.concatenate(
            [
                jnp.concatenate(
                    [held[pl.ds(g * WHOLE + j * 2 + s, half, stride=UNIT), :] for j in range(UNIT // 2)], axis=1
                )
                for s in range(2)
            ],
            axis=0,
        )

    right = (r, lax.rem(c + 1, COLS))
    for g in range(GROUPS):
        pltpu.make_async_remote_copy(
            x_ref.at[most], held.at[most], there_send, there_recv.at[g], device_id=right, device_id_type=MESH
        ).wait_recv()
        matrix = rows_of(g)
        grams[g, c] = product(matrix, matrix, 1)
        for step in range(1, COLS):
            pltpu.make_async_remote_copy(
                grams.at[g, c], grams.at[g, c], gram_send, gram_recv.at[g],
                device_id=(r, lax.rem(c + step, COLS)), device_id_type=MESH,
            ).start()
        pltpu.make_async_remote_copy(
            grams.at[g, pl.ds(0, COLS - 1)], grams.at[g, pl.ds(0, COLS - 1)], gram_send, gram_recv.at[g],
            device_id=right, device_id_type=MESH,
        ).wait_recv()
        gram = (grams[g, 0] + grams[g, 1]) + (grams[g, 2] + grams[g, 3])
        scale = lax.rsqrt(jnp.sum(jnp.where(diagonal, gram, 0.0), axis=(0, 1), keepdims=True) + 1e-06)
        gram = (gram * scale) * scale
        total = None
        for step in range(ITERS):
            mixed = -4.775 * gram + 2.0315 * product(gram, gram)
            if step == 0:
                total = jnp.where(diagonal, 3.4445, 0.0) + mixed
            else:
                total = 3.4445 * total + product(mixed, total)
            if step < ITERS - 1:
                gram = 3.4445 * gram + product(mixed, gram)
                gram = 3.4445 * gram + product(mixed, gram)
        result = product(total * scale, matrix)
        for s in range(2):
            for j in range(UNIT // 2):
                done[pl.ds(g * WHOLE + j * 2 + s, half, stride=UNIT), :] = result[
                    s * half : (s + 1) * half, j * LANES : (j + 1) * LANES
                ]

        def again(i, carry):
            p = partner(i)
            pltpu.make_async_remote_copy(
                done.at[unit(g * WHOLE + p * UNIT)],
                back_ref.at[unit((r * GROUPS + g) * UNIT)],
                back_send, back_recv,
                device_id=(p, c), device_id_type=MESH,
            ).start()
            return carry

        lax.fori_loop(1, ROWS, again, 0)
        back_ref[unit((r * GROUPS + g) * UNIT), :] = done[unit(g * WHOLE + r * UNIT), :]

    whole = pl.ds(0, (ROWS - 1) * UNIT * GROUPS)
    pltpu.make_async_remote_copy(
        x_ref.at[whole], held.at[whole], there_send, back_recv, device_id=right, device_id_type=MESH
    ).wait()
    pltpu.make_async_remote_copy(
        done.at[whole], back_ref.at[whole], back_send, back_recv, device_id=right, device_id_type=MESH
    ).wait_send()
    sent = grams.at[pl.ds(0, COLS - 1)]
    pltpu.make_async_remote_copy(
        sent, sent, gram_send, back_recv, device_id=right, device_id_type=MESH
    ).wait_send()


def flat(x):
    return x.reshape(256, 2, 8, 128).transpose(0, 2, 1, 3).reshape(4096, 128)


def unflat(x):
    return x.reshape(256, 8, 2, 128).transpose(0, 2, 1, 3).reshape(256, 2, 1024)


def local(gradients, momentum, weights):
    new_momentum = hold_rate * momentum + gradients
    shape = (ROWS * GROUPS * UNIT, LANES)
    back = pl.pallas_call(
        kernel,
        name="orthogonal",
        out_shape=jax.ShapeDtypeStruct(shape, jnp.float32),
        in_specs=[pl.BlockSpec(memory_space=pltpu.VMEM)],
        out_specs=pl.BlockSpec(memory_space=pltpu.VMEM),
        scratch_shapes=[
            pltpu.VMEM(shape, jnp.float32),
            pltpu.VMEM((GROUPS, COLS, SIDE, SIDE), jnp.float32),
            pltpu.VMEM(shape, jnp.float32),
            pltpu.SemaphoreType.DMA,
            pltpu.SemaphoreType.DMA((GROUPS,)),
            pltpu.SemaphoreType.DMA,
            pltpu.SemaphoreType.DMA((GROUPS,)),
            pltpu.SemaphoreType.DMA,
            pltpu.SemaphoreType.DMA,
        ],
        compiler_params=pltpu.CompilerParams(collective_id=0, has_side_effects=True),
    )(flat(new_momentum))
    new_weights = (1.0 - learn_rate * decay_rate) * weights - learn_rate * unflat(back)
    return (new_weights, new_momentum)


def solution(mesh):
    placed = (P(None, "rows", "cols"), P(None, "rows", "cols"), P(None, "rows", "cols"))
    return jax.shard_map(
        local,
        mesh=mesh,
        in_specs=placed,
        out_specs=(P(None, "rows", "cols"), P(None, "rows", "cols")),
        check_vma=False,
    )
```

time: 230 us -> 120 us (0.52)
  blocking collectives: 180 us -> 0 us
  Pallas kernels: 0 us -> 108 us
  local copies, waits for them, and re-layouts: 18.6 us -> 0.29 us
  matrix products: 17.9 us -> 0 us
    all_to_all x4 -> x0, blocking collectives: 180 us -> none  [the longest x1 63.3 us: local(): lax.all_to_all(new_momentum, 'rows', split_axis=0, concat_axis=1, tiled=T...]
    pallas_call x0 -> x1, Pallas kernels: none -> 108 us  [local(): pl.pallas_call(kernel, name='orthogonal', out_shape=jax.ShapeDtypeStruct(...]
    dot_general x12 -> x0, matrix products: 17.9 us -> none  [the longest x4 9.94 us: local(): jnp.einsum('mij,mjk->mik', mixed, iterate, precision=lax.Precision.HIGHEST)]
    mul x4 -> x0, local copies, waits for them, and re-layouts: 9.68 us -> none  [the longest x2 5.84 us: local(): 3.4445 * iterate]
    all_to_all x3 -> x0, local copies, waits for them, and re-layouts: 5.2 us -> none  [the longest x2 3.24 us: local(): lax.all_to_all(new_momentum, 'rows', split_axis=0, concat_axis=1, tiled=T...]
    add x1 -> x0, local copies, waits for them, and re-layouts: 3.7 us -> none  [local(): 3.4445 * iterate]
where the time goes in v1:
time: 120 us; the launch traced here: 119 us
  Pallas kernels  108 us (90%)
  other arithmetic  9.66 us (8%)
    pallas_call x1, Pallas kernels, local(): pl.pallas_call(kernel, name='orthogonal', out_shape=jax.ShapeDtypeStruct(...  108 us
    add x1, other arithmetic, local(): new_momentum = hold_rate * momentum + gradients  4.98 us
    sub x1, other arithmetic, local(): (1.0 - learn_rate * decay_rate) * weights - learn_rate * unflat(back)  2.76 us

profile of v1, /device:TPU:1, one launch (start us, length us, event | category | flops | bytes accessed | tf_op | source)
XLA Modules:
  0.0 119.0 jit_solution(430981934208748852)
XLA Ops:
  0.6 5.0 %multiply_add_fusion = f32[256,2,1024]{2,1,0:T(2,128)} fusion(f32[256,2,1024]{2,1,0:T(2,128)} %param.3, f32[256,2,1024]{2,1,0:T(2,128)} %param.4), kind=kLoop, calls=%fused_computation | loop fusion | flops 1048576 | bytes 6291456 | tf_op jit(solution)/shard_map/add | solution.py:160
  5.6 108.4 %orthogonal.1 = f32[4096,128]{1,0:T(8,128)} custom-call(f32[4096,128]{1,0:T(8,128)} %bitcast.10), custom_call_target="tpu_custom_call" | custom-call | tf_op jit(solution)/shard_map/orthogonal/pallas_call | solution.py:162
  114.0 0.0 copy-start
  114.0 1.9 %broadcast_multiply_fusion = f32[4096,128]{1,0:T(8,128)S(1)} fusion(f32[4096,128]{1,0:T(8,128)} %orthogonal.1), kind=kLoop, calls=%fused_computation.2 | loop fusion | flops 524288 | bytes 4194304 | tf_op jit(solution)/shard_map/mul | solution.py:181
  115.9 0.3 copy-done
  116.2 2.8 %multiply_subtract_fusion = f32[256,2,1024]{2,1,0:T(2,128)} fusion(f32[256,2,1024]{2,1,0:T(2,128)S(1)} %bitcast.11, f32[256,2,1024]{2,1,0:T(2,128)S(1)} %copy-done), kind=kLoop, calls=%fused_computation.1 | loop fusion | flops 1048576 | bytes 6291456 | tf_op jit(solution)/shard_map/sub | solution.py:181
Async XLA Ops:
  114.0 2.2 %copy-start = (f32[256,2,1024]{2,1,0:T(2,128)S(1)}, f32[256,2,1024]{2,1,0:T(2,128)}, u32[]{:S(2)}) copy-start(f32[256,2,1024]{2,1,0:T(2,128)} %param.5) | copy-start | bytes 6291460

commit v2 on v1

--- a/solution.py
+++ b/solution.py
@@ -15,6 +15,7 @@
 UNIT = 16
 WHOLE = ROWS * UNIT
 MESH = pl.DeviceIdType.MESH
+VMEM_LIMIT = 24 * 1024 * 1024
 
 hold_rate = 0.8
 learn_rate = 0.8
@@ -28,46 +29,71 @@
     )
 
 
-def kernel(x_ref, back_ref, held, grams, done, there_send, there_recv, gram_send, gram_recv, back_send, back_recv):
+def kernel(
+    g_ref, m_ref, w_ref, back_ref, x_ref,
+    held, grams, done, g_buf, m_buf, w_buf,
+    load_sem, weight_sem, there_send, there_recv, gram_send, gram_recv, back_send, back_recv,
+):
     r = lax.axis_index("rows")
     c = lax.axis_index("cols")
     z, y, k = r // (Y * CORES), (r // CORES) % Y, r % CORES
 
-    def partner(i):
-        return (
-            lax.rem(z + i % Z, Z) * (Y * CORES)
-            + lax.rem(y + (i // Z) % Y, Y) * CORES
-            + lax.rem(k + i // (Z * Y), CORES)
-        )
+    along_z = [lax.rem(z + dz, Z) * (Y * CORES) for dz in range(Z)]
+
+    def for_partners(act):
+        def some(dy, dk, first):
+            near = lax.rem(y + dy, Y) * CORES + lax.rem(k + dk, CORES)
+            for dz in range(first, Z):
+                act(along_z[dz] + near)
+
+        def body(i, carry):
+            some(i % Y, i // Y, 0)
+            return carry
+
+        some(0, 0, 1)
+        lax.fori_loop(1, Y * CORES, body, 0)
+
+    def unit(start):
+        return pl.ds(pl.multiple_of(start, UNIT), UNIT)
+
+    def chunk(g):
+        return pl.ds(g * WHOLE, WHOLE)
 
     barrier = pltpu.get_barrier_semaphore()
 
-    def greet(i, carry):
-        pl.semaphore_signal(barrier, inc=1, device_id=(partner(i), c), device_id_type=MESH)
-        return carry
-
-    lax.fori_loop(1, ROWS, greet, 0)
+    loads = []
+    for g in range(GROUPS):
+        pair = [
+            pltpu.make_async_copy(g_ref.at[chunk(g)], g_buf.at[chunk(g)], load_sem.at[0, g]),
+            pltpu.make_async_copy(m_ref.at[chunk(g)], m_buf.at[chunk(g)], load_sem.at[1, g]),
+        ]
+        for copy in pair:
+            copy.start()
+        loads.append(pair)
+    for_partners(lambda p: pl.semaphore_signal(barrier, inc=1, device_id=(p, c), device_id_type=MESH))
     for step in range(1, COLS):
         pl.semaphore_signal(barrier, inc=1, device_id=(r, lax.rem(c + step, COLS)), device_id_type=MESH)
+
+    for g in range(GROUPS):
+        for copy in loads[g]:
+            copy.wait()
+        x_ref[chunk(g), :] = hold_rate * m_buf[chunk(g), :] + g_buf[chunk(g), :]
     pl.semaphore_wait(barrier, ROWS - 1 + COLS - 1)
 
-    def unit(start):
-        return pl.ds(pl.multiple_of(start, UNIT), UNIT)
-
-    for g in range(GROUPS):
-        def there(i, carry):
-            p = partner(i)
-            pltpu.make_async_remote_copy(
-                x_ref.at[unit((p * GROUPS + g) * UNIT)],
-                held.at[unit(g * WHOLE + r * UNIT)],
+    for g in range(GROUPS):
+        for_partners(
+            lambda p: pltpu.make_async_remote_copy(
+                x_ref.at[unit((g * ROWS + p) * UNIT)],
+                held.at[unit((g * ROWS + r) * UNIT)],
                 there_send, there_recv.at[g],
                 device_id=(p, c), device_id_type=MESH,
             ).start()
-            return carry
-
-        lax.fori_loop(1, ROWS, there, 0)
-    for g in range(GROUPS):
-        held[unit(g * WHOLE + r * UNIT), :] = x_ref[unit((r * GROUPS + g) * UNIT), :]
+        )
+    weights = pltpu.make_async_copy(w_ref, w_buf, weight_sem)
+    weights.start()
+    for g in range(GROUPS):
+        own = unit((g * ROWS + r) * UNIT)
+        held[own, :] = x_ref[own, :]
 
     row = lax.broadcasted_iota(jnp.int32, (SIDE, SIDE), 0)
     col = lax.broadcasted_iota(jnp.int32, (SIDE, SIDE), 1)
@@ -122,30 +148,46 @@
                     s * half : (s + 1) * half, j * LANES : (j + 1) * LANES
                 ]
 
-        def again(i, carry):
-            p = partner(i)
-            pltpu.make_async_remote_copy(
-                done.at[unit(g * WHOLE + p * UNIT)],
-                back_ref.at[unit((r * GROUPS + g) * UNIT)],
-                back_send, back_recv,
+        for_partners(
+            lambda p: pltpu.make_async_remote_copy(
+                done.at[unit((g * ROWS + p) * UNIT)],
+                back_ref.at[unit((g * ROWS + r) * UNIT)],
+                back_send, back_recv.at[g],
                 device_id=(p, c), device_id_type=MESH,
             ).start()
-            return carry
-
-        lax.fori_loop(1, ROWS, again, 0)
-        back_ref[unit((r * GROUPS + g) * UNIT), :] = done[unit(g * WHOLE + r * UNIT), :]
+        )
+        own = unit((g * ROWS + r) * UNIT)
+        back_ref[own, :] = done[own, :]
+
+    weights.wait()
+    for g in range(GROUPS):
+        pltpu.make_async_remote_copy(
+            x_ref.at[most], back_ref.at[most], there_send, back_recv.at[g], device_id=right, device_id_type=MESH
+        ).wait_recv()
+        back_ref[chunk(g), :] = (1.0 - learn_rate * decay_rate) * w_buf[chunk(g), :] - learn_rate * back_ref[chunk(g), :]
 
     whole = pl.ds(0, (ROWS - 1) * UNIT * GROUPS)
     pltpu.make_async_remote_copy(
-        x_ref.at[whole], held.at[whole], there_send, back_recv, device_id=right, device_id_type=MESH
-    ).wait()
+        x_ref.at[whole], held.at[whole], there_send, there_recv.at[0], device_id=right, device_id_type=MESH
+    ).wait_send()
     pltpu.make_async_remote_copy(
-        done.at[whole], back_ref.at[whole], back_send, back_recv, device_id=right, device_id_type=MESH
+        done.at[whole], back_ref.at[whole], back_send, back_recv.at[0], device_id=right, device_id_type=MESH
     ).wait_send()
     sent = grams.at[pl.ds(0, COLS - 1)]
     pltpu.make_async_remote_copy(
-        sent, sent, gram_send, back_recv, device_id=right, device_id_type=MESH
+        sent, sent, gram_send, gram_recv.at[0], device_id=right, device_id_type=MESH
     ).wait_send()
+
+
+def write(weights, momentum, weights_out, momentum_out, sems):
+    copies = [
+        pltpu.make_async_copy(weights, weights_out, sems.at[0]),
+        pltpu.make_async_copy(momentum, momentum_out, sems.at[1]),
+    ]
+    for copy in copies:
+        copy.start()
+    for copy in copies:
+        copy.wait()
 
 
 def flat(x):
@@ -157,29 +199,41 @@
 
 
 def local(gradients, momentum, weights):
-    new_momentum = hold_rate * momentum + gradients
     shape = (ROWS * GROUPS * UNIT, LANES)
-    back = pl.pallas_call(
+    new_weights, new_momentum = pl.pallas_call(
         kernel,
         name="orthogonal",
-        out_shape=jax.ShapeDtypeStruct(shape, jnp.float32),
-        in_specs=[pl.BlockSpec(memory_space=pltpu.VMEM)],
-        out_specs=pl.BlockSpec(memory_space=pltpu.VMEM),
+        out_shape=[jax.ShapeDtypeStruct(shape, jnp.float32)] * 2,
+        in_specs=[pl.BlockSpec(memory_space=pltpu.HBM)] * 3,
+        out_specs=[pl.BlockSpec(memory_space=pltpu.VMEM)] * 2,
         scratch_shapes=[
             pltpu.VMEM(shape, jnp.float32),
             pltpu.VMEM((GROUPS, COLS, SIDE, SIDE), jnp.float32),
             pltpu.VMEM(shape, jnp.float32),
+            pltpu.VMEM(shape, jnp.float32),
+            pltpu.VMEM(shape, jnp.float32),
+            pltpu.VMEM(shape, jnp.float32),
+            pltpu.SemaphoreType.DMA((2, GROUPS)),
+            pltpu.SemaphoreType.DMA,
             pltpu.SemaphoreType.DMA,
             pltpu.SemaphoreType.DMA((GROUPS,)),
             pltpu.SemaphoreType.DMA,
             pltpu.SemaphoreType.DMA((GROUPS,)),
             pltpu.SemaphoreType.DMA,
-            pltpu.SemaphoreType.DMA,
+            pltpu.SemaphoreType.DMA((GROUPS,)),
         ],
-        compiler_params=pltpu.CompilerParams(collective_id=0, has_side_effects=True),
-    )(flat(new_momentum))
-    new_weights = (1.0 - learn_rate * decay_rate) * weights - learn_rate * unflat(back)
-    return (new_weights, new_momentum)
+        compiler_params=pltpu.CompilerParams(collective_id=0, has_side_effects=True, vmem_limit_bytes=VMEM_LIMIT),
+    )(*(pltpu.with_memory_space_constraint(flat(x), pltpu.HBM) for x in (gradients, momentum, weights)))
+    new_weights, new_momentum = pl.pallas_call(
+        write,
+        name="write",
+        out_shape=[jax.ShapeDtypeStruct(shape, jnp.float32)] * 2,
+        in_specs=[pl.BlockSpec(memory_space=pltpu.VMEM)] * 2,
+        out_specs=[pl.BlockSpec(memory_space=pltpu.HBM)] * 2,
+        scratch_shapes=[pltpu.SemaphoreType.DMA((2,))],
+        compiler_params=pltpu.CompilerParams(vmem_limit_bytes=8 * 1024 * 1024),
+    )(new_weights, new_momentum)
+    return (unflat(new_weights), unflat(new_momentum))
 
 
 def solution(mesh):

time: 120 us -> 107 us (0.89); the launches traced: 119 us -> 107 us
  other arithmetic: 9.66 us -> 0 us
    add x1 -> x0, other arithmetic: 4.98 us -> none  [local(): new_momentum = hold_rate * momentum + gradients]
    sub x1 -> x0, other arithmetic: 2.76 us -> none  [local(): (1.0 - learn_rate * decay_rate) * weights - learn_rate * unflat(back)]
    mul x1 -> x0, other arithmetic: 1.92 us -> none  [local(): learn_rate * unflat(back)]
    pallas_call x1 -> x2, Pallas kernels: 108 us -> 107 us  [the longest x1 105 us: local(): pl.pallas_call(kernel, name='orthogonal', out_shape=[jax.ShapeDtypeStruct...]
where the time goes in v2:
time: 107 us
  Pallas kernels  107 us (100%)
    pallas_call x1, Pallas kernels, local(): pl.pallas_call(kernel, name='orthogonal', out_shape=[jax.ShapeDtypeStruct...  105 us

profile of v2, /device:TPU:1, one launch (start us, length us, event | category | flops | bytes accessed | tf_op | source)
XLA Modules:
  0.0 107.3 jit_solution(7941647070893189927)
XLA Ops:
  0.6 104.6 %orthogonal.1 = (f32[4096,128]{1,0:T(8,128)S(1)}, f32[4096,128]{1,0:T(8,128)S(1)}) custom-call(f32[4096,128]{1,0:T(8,128)} %bitcast.25, f32[4096,128]{1,0:T(8,128)} %bitcast.26, f32[4096,128]{1,0:T(8,128)} %bitcast.27), custom_call_target="tpu_custom_call" | custom-call | tf_op jit(solution)/shard_map/orthogonal/pallas_call | solution.py:203
  105.2 2.0 %write.1 = (f32[4096,128]{1,0:T(8,128)}, f32[4096,128]{1,0:T(8,128)}) custom-call(f32[4096,128]{1,0:T(8,128)S(1)} %get-tuple-element.6.weights, f32[4096,128]{1,0:T(8,128)S(1)} %get-tuple-element.7.momentum), custom_call_target="tpu_custom_call" | custom-call | tf_op jit(solution)/shard_map/write/pallas_call | solution.py:227

commit v3 on v2

--- a/solution.py
+++ b/solution.py
@@ -32,7 +32,7 @@
 def kernel(
     g_ref, m_ref, w_ref, back_ref, x_ref,
     held, grams, done, g_buf, m_buf, w_buf,
-    load_sem, weight_sem, there_send, there_recv, gram_send, gram_recv, back_send, back_recv,
+    here, load_sem, weight_sem, there_send, there_recv, gram_send, gram_recv, back_send, back_recv,
 ):
     r = lax.axis_index("rows")
     c = lax.axis_index("cols")
@@ -40,18 +40,29 @@
 
     along_z = [lax.rem(z + dz, Z) * (Y * CORES) for dz in range(Z)]
 
-    def for_partners(act):
-        def some(dy, dk, first):
-            near = lax.rem(y + dy, Y) * CORES + lax.rem(k + dk, CORES)
-            for dz in range(first, Z):
-                act(along_z[dz] + near)
-
+    def some(act, dy, dk, steps):
+        near = lax.rem(y + dy, Y) * CORES + lax.rem(k + dk, CORES)
+        for dz in steps:
+            act(along_z[dz] + near)
+
+    def for_near(act, steps):
         def body(i, carry):
-            some(i % Y, i // Y, 0)
+            some(act, i % Y, i // Y, steps)
             return carry
 
-        some(0, 0, 1)
+        some(act, 0, 0, [dz for dz in steps if dz])
         lax.fori_loop(1, Y * CORES, body, 0)
+
+    def for_all(act):
+        steps = (4, 5, 3, 6, 2, 7, 1, 0)
+
+        def body(i, carry):
+            upper, lower = i // 4, i // 2 % 2
+            some(act, 2 + upper - lower - 2 * upper * lower, 1 - i % 2, steps)
+            return carry
+
+        lax.fori_loop(0, Y * CORES - 1, body, 0)
+        some(act, 0, 0, steps[:-1])
 
     def unit(start):
         return pl.ds(pl.multiple_of(start, UNIT), UNIT)
@@ -70,25 +81,51 @@
         for copy in pair:
             copy.start()
         loads.append(pair)
-    for_partners(lambda p: pl.semaphore_signal(barrier, inc=1, device_id=(p, c), device_id_type=MESH))
+    def signal(semaphore, device):
+        pl.semaphore_signal(semaphore, inc=1, device_id=(device, c), device_id_type=MESH)
+
+    for_near(lambda p: signal(barrier, p), (1, 7, 0))
     for step in range(1, COLS):
         pl.semaphore_signal(barrier, inc=1, device_id=(r, lax.rem(c + step, COLS)), device_id_type=MESH)
 
-    for g in range(GROUPS):
-        for copy in loads[g]:
-            copy.wait()
-        x_ref[chunk(g), :] = hold_rate * m_buf[chunk(g), :] + g_buf[chunk(g), :]
-    pl.semaphore_wait(barrier, ROWS - 1 + COLS - 1)
-
-    for g in range(GROUPS):
-        for_partners(
+    def there(g, steps):
+        for_near(
             lambda p: pltpu.make_async_remote_copy(
                 x_ref.at[unit((g * ROWS + p) * UNIT)],
                 held.at[unit((g * ROWS + r) * UNIT)],
                 there_send, there_recv.at[g],
                 device_id=(p, c), device_id_type=MESH,
-            ).start()
+            ).start(),
+            steps,
         )
+
+    def add(g):
+        for copy in loads[g]:
+            copy.wait()
+        x_ref[chunk(g), :] = hold_rate * m_buf[chunk(g), :] + g_buf[chunk(g), :]
+
+    def tell(stage):
+        for dz in (1, Z - 1):
+            signal(here.at[stage], along_z[dz] + y * CORES + k)
+
+    add(0)
+    pl.semaphore_wait(barrier, 3 * Y * CORES - 1 + COLS - 1)
+    tell(0)
+    there(0, (1, 7, 0))
+    add(1)
+    there(1, (1, 7, 0))
+    pl.semaphore_wait(here.at[0], 2)
+    tell(1)
+    there(0, (2, 6))
+    pl.semaphore_wait(here.at[1], 2)
+    tell(2)
+    there(0, (3, 5))
+    pl.semaphore_wait(here.at[2], 2)
+    there(0, (4,))
+    there(1, (2, 6, 3, 5, 4))
+    for g in range(2, GROUPS):
+        add(g)
+        there(g, (1, 7, 2, 6, 3, 5, 4, 0))
     weights = pltpu.make_async_copy(w_ref, w_buf, weight_sem)
     weights.start()
     for g in range(GROUPS):
@@ -148,7 +185,7 @@
                     s * half : (s + 1) * half, j * LANES : (j + 1) * LANES
                 ]
 
-        for_partners(
+        for_all(
             lambda p: pltpu.make_async_remote_copy(
                 done.at[unit((g * ROWS + p) * UNIT)],
                 back_ref.at[unit((g * ROWS + r) * UNIT)],
@@ -213,6 +250,7 @@
             pltpu.VMEM(shape, jnp.float32),
             pltpu.VMEM(shape, jnp.float32),
             pltpu.VMEM(shape, jnp.float32),
+            pltpu.SemaphoreType.REGULAR((3,)),
             pltpu.SemaphoreType.DMA((2, GROUPS)),
             pltpu.SemaphoreType.DMA,
             pltpu.SemaphoreType.DMA,

time: 107 us -> 106 us (level)
  Pallas kernels: 107 us -> 105 us
    pallas_call x1, Pallas kernels: 105 us -> 103 us  [local(): pl.pallas_call(kernel, name='orthogonal', out_shape=[jax.ShapeDtypeStruct...]
where the time goes in v3:
time: 106 us
  Pallas kernels  105 us (99%)
    pallas_call x1, Pallas kernels, local(): pl.pallas_call(kernel, name='orthogonal', out_shape=[jax.ShapeDtypeStruct...  103 us

profile of v3, /device:TPU:1, one launch (start us, length us, event | category | flops | bytes accessed | tf_op | source)
XLA Modules:
  0.0 105.6 jit_solution(2586351774463245323)
XLA Ops:
  0.6 102.9 %orthogonal.1 = (f32[4096,128]{1,0:T(8,128)S(1)}, f32[4096,128]{1,0:T(8,128)S(1)}) custom-call(f32[4096,128]{1,0:T(8,128)} %bitcast.25, f32[4096,128]{1,0:T(8,128)} %bitcast.26, f32[4096,128]{1,0:T(8,128)} %bitcast.27), custom_call_target="tpu_custom_call" | custom-call | tf_op jit(solution)/shard_map/orthogonal/pallas_call | solution.py:240
  103.6 2.0 %write.1 = (f32[4096,128]{1,0:T(8,128)}, f32[4096,128]{1,0:T(8,128)}) custom-call(f32[4096,128]{1,0:T(8,128)S(1)} %get-tuple-element.6.weights, f32[4096,128]{1,0:T(8,128)S(1)} %get-tuple-element.7.momentum), custom_call_target="tpu_custom_call" | custom-call | tf_op jit(solution)/shard_map/write/pallas_call | solution.py:265

commit v4 on v3

--- a/solution.py
+++ b/solution.py
@@ -15,6 +15,7 @@
 UNIT = 16
 WHOLE = ROWS * UNIT
 MESH = pl.DeviceIdType.MESH
+EARLY_Z = (0, 4, 1, 5, 2, 6, 3, 7)
 VMEM_LIMIT = 24 * 1024 * 1024
 
 hold_rate = 0.8
@@ -53,7 +54,7 @@
         some(act, 0, 0, [dz for dz in steps if dz])
         lax.fori_loop(1, Y * CORES, body, 0)
 
-    def for_all(act):
+    def for_all(act, level=0):
         steps = (4, 5, 3, 6, 2, 7, 1, 0)
 
         def body(i, carry):
@@ -61,8 +62,19 @@
             some(act, 2 + upper - lower - 2 * upper * lower, 1 - i % 2, steps)
             return carry
 
-        lax.fori_loop(0, Y * CORES - 1, body, 0)
-        some(act, 0, 0, steps[:-1])
+        lax.fori_loop(0, Y * CORES - max(level, 1), body, 0)
+        if not level:
+            some(act, 0, 0, steps[:-1])
+            return
+        lasts = [(2, 1), (2, 0), (1, 1), (1, 0), (3, 1), (3, 0), (0, 1), (0, 0)][-level:]
+        near = [lax.rem(y + dy, Y) * CORES + lax.rem(k + dk, CORES) for dy, dk in lasts]
+        for there_z in EARLY_Z:
+            for last, (dy, dk) in zip(near, lasts):
+                device = there_z * (Y * CORES) + last
+                if (dy, dk) == (0, 0):
+                    pl.when(device != r)(lambda device=device: act(device))
+                else:
+                    act(device)
 
     def unit(start):
         return pl.ds(pl.multiple_of(start, UNIT), UNIT)
@@ -191,7 +203,8 @@
                 back_ref.at[unit((g * ROWS + r) * UNIT)],
                 back_send, back_recv.at[g],
                 device_id=(p, c), device_id_type=MESH,
-            ).start()
+            ).start(),
+            4 if g == GROUPS - 1 else 0,
         )
         own = unit((g * ROWS + r) * UNIT)
         back_ref[own, :] = done[own, :]

time: 106 us -> 104 us (0.981)
  Pallas kernels: 105 us -> 103 us
    pallas_call x1, Pallas kernels: 103 us -> 101 us  [local(): pl.pallas_call(kernel, name='orthogonal', out_shape=[jax.ShapeDtypeStruct...]
where the time goes in v4:
time: 104 us
  Pallas kernels  103 us (99%)
    pallas_call x1, Pallas kernels, local(): pl.pallas_call(kernel, name='orthogonal', out_shape=[jax.ShapeDtypeStruct...  101 us

profile of v4, /device:TPU:1, one launch (start us, length us, event | category | flops | bytes accessed | tf_op | source)
XLA Modules:
  0.0 104.1 jit_solution(17159139334829761761)
XLA Ops:
  0.6 101.4 %orthogonal.1 = (f32[4096,128]{1,0:T(8,128)S(1)}, f32[4096,128]{1,0:T(8,128)S(1)}) custom-call(f32[4096,128]{1,0:T(8,128)} %bitcast.25, f32[4096,128]{1,0:T(8,128)} %bitcast.26, f32[4096,128]{1,0:T(8,128)} %bitcast.27), custom_call_target="tpu_custom_call" | custom-call | tf_op jit(solution)/shard_map/orthogonal/pallas_call | solution.py:253
  102.0 2.0 %write.1 = (f32[4096,128]{1,0:T(8,128)}, f32[4096,128]{1,0:T(8,128)}) custom-call(f32[4096,128]{1,0:T(8,128)S(1)} %get-tuple-element.6.weights, f32[4096,128]{1,0:T(8,128)S(1)} %get-tuple-element.7.momentum), custom_call_target="tpu_custom_call" | custom-call | tf_op jit(solution)/shard_map/write/pallas_call | solution.py:278

commit v5 on v4

--- a/solution.py
+++ b/solution.py
@@ -84,6 +84,15 @@
 
     barrier = pltpu.get_barrier_semaphore()
 
+    def signal(semaphore, device):
+        pl.semaphore_signal(semaphore, inc=1, device_id=(device, c), device_id_type=MESH)
+
+    for step in (2, 1, 3):
+        pl.semaphore_signal(barrier, inc=1, device_id=(r, lax.rem(c + step, COLS)), device_id_type=MESH)
+    for dy in (2, 1, 3, 0):
+        for dk in (1, 0):
+            some(lambda p: signal(barrier, p), dy, dk, (1, 7, 0) if dy or dk else (1, 7))
+
     loads = []
     for g in range(GROUPS):
         pair = [
@@ -93,12 +102,6 @@
         for copy in pair:
             copy.start()
         loads.append(pair)
-    def signal(semaphore, device):
-        pl.semaphore_signal(semaphore, inc=1, device_id=(device, c), device_id_type=MESH)
-
-    for_near(lambda p: signal(barrier, p), (1, 7, 0))
-    for step in range(1, COLS):
-        pl.semaphore_signal(barrier, inc=1, device_id=(r, lax.rem(c + step, COLS)), device_id_type=MESH)
 
     def there(g, steps):
         for_near(
@@ -209,6 +212,14 @@
         own = unit((g * ROWS + r) * UNIT)
         back_ref[own, :] = done[own, :]
 
+    whole = pl.ds(0, (ROWS - 1) * UNIT * GROUPS)
+    pltpu.make_async_remote_copy(
+        x_ref.at[whole], held.at[whole], there_send, there_recv.at[0], device_id=right, device_id_type=MESH
+    ).wait_send()
+    sent = grams.at[pl.ds(0, COLS - 1)]
+    pltpu.make_async_remote_copy(
+        sent, sent, gram_send, gram_recv.at[0], device_id=right, device_id_type=MESH
+    ).wait_send()
     weights.wait()
     for g in range(GROUPS):
         pltpu.make_async_remote_copy(
@@ -216,16 +227,8 @@
         ).wait_recv()
         back_ref[chunk(g), :] = (1.0 - learn_rate * decay_rate) * w_buf[chunk(g), :] - learn_rate * back_ref[chunk(g), :]
 
-    whole = pl.ds(0, (ROWS - 1) * UNIT * GROUPS)
-    pltpu.make_async_remote_copy(
-        x_ref.at[whole], held.at[whole], there_send, there_recv.at[0], device_id=right, device_id_type=MESH
-    ).wait_send()
     pltpu.make_async_remote_copy(
         done.at[whole], back_ref.at[whole], back_send, back_recv.at[0], device_id=right, device_id_type=MESH
-    ).wait_send()
-    sent = grams.at[pl.ds(0, COLS - 1)]
-    pltpu.make_async_remote_copy(
-        sent, sent, gram_send, gram_recv.at[0], device_id=right, device_id_type=MESH
     ).wait_send()
 
 

time: 104 us -> 104 us (level)
  no operation moved by 1% of the time
where the time goes in v5:
time: 104 us
  Pallas kernels  104 us (100%)
    pallas_call x1, Pallas kernels, local(): pl.pallas_call(kernel, name='orthogonal', out_shape=[jax.ShapeDtypeStruct...  102 us

profile of v5, /device:TPU:1, one launch (start us, length us, event | category | flops | bytes accessed | tf_op | source)
XLA Modules:
  0.0 104.3 jit_solution(4367256894720162799)
XLA Ops:
  0.6 101.6 %orthogonal.1 = (f32[4096,128]{1,0:T(8,128)S(1)}, f32[4096,128]{1,0:T(8,128)S(1)}) custom-call(f32[4096,128]{1,0:T(8,128)} %bitcast.25, f32[4096,128]{1,0:T(8,128)} %bitcast.26, f32[4096,128]{1,0:T(8,128)} %bitcast.27), custom_call_target="tpu_custom_call" | custom-call | tf_op jit(solution)/shard_map/orthogonal/pallas_call | solution.py:256
  102.3 2.0 %write.1 = (f32[4096,128]{1,0:T(8,128)}, f32[4096,128]{1,0:T(8,128)}) custom-call(f32[4096,128]{1,0:T(8,128)S(1)} %get-tuple-element.6.weights, f32[4096,128]{1,0:T(8,128)S(1)} %get-tuple-element.7.momentum), custom_call_target="tpu_custom_call" | custom-call | tf_op jit(solution)/shard_map/write/pallas_call | solution.py:281

commit v6 on v3

--- a/solution.py
+++ b/solution.py
@@ -15,6 +15,7 @@
 UNIT = 16
 WHOLE = ROWS * UNIT
 MESH = pl.DeviceIdType.MESH
+EARLY_Z = (0, 4, 1, 5, 2, 6, 3, 7)
 VMEM_LIMIT = 24 * 1024 * 1024
 
 hold_rate = 0.8
@@ -53,7 +54,7 @@
         some(act, 0, 0, [dz for dz in steps if dz])
         lax.fori_loop(1, Y * CORES, body, 0)
 
-    def for_all(act):
+    def for_all(act, last=False):
         steps = (4, 5, 3, 6, 2, 7, 1, 0)
 
         def body(i, carry):
@@ -61,8 +62,22 @@
             some(act, 2 + upper - lower - 2 * upper * lower, 1 - i % 2, steps)
             return carry
 
-        lax.fori_loop(0, Y * CORES - 1, body, 0)
-        some(act, 0, 0, steps[:-1])
+        def others(device):
+            pl.when(device != r)(lambda: act(device))
+
+        def low(i, carry):
+            for dz in steps:
+                others(along_z[dz] + i)
+            return carry
+
+        if last:
+            lax.fori_loop(0, CORES, low, 0)
+            for there_z in EARLY_Z:
+                for near in range(CORES, Y * CORES):
+                    others(there_z * (Y * CORES) + near)
+        else:
+            lax.fori_loop(0, Y * CORES - 1, body, 0)
+            some(act, 0, 0, steps[:-1])
 
     def unit(start):
         return pl.ds(pl.multiple_of(start, UNIT), UNIT)
@@ -191,7 +206,8 @@
                 back_ref.at[unit((g * ROWS + r) * UNIT)],
                 back_send, back_recv.at[g],
                 device_id=(p, c), device_id_type=MESH,
-            ).start()
+            ).start(),
+            g == GROUPS - 1,
         )
         own = unit((g * ROWS + r) * UNIT)
         back_ref[own, :] = done[own, :]

time: 106 us -> 105 us (level); the launches traced: 106 us -> 103 us
  Pallas kernels: 105 us -> 103 us
    pallas_call x1, Pallas kernels: 103 us -> 101 us  [local(): pl.pallas_call(kernel, name='orthogonal', out_shape=[jax.ShapeDtypeStruct...]
where the time goes in v6:
time: 105 us; the launch traced here: 103 us
  Pallas kernels  103 us (98%)
    pallas_call x1, Pallas kernels, local(): pl.pallas_call(kernel, name='orthogonal', out_shape=[jax.ShapeDtypeStruct...  101 us

profile of v6, /device:TPU:1, one launch (start us, length us, event | category | flops | bytes accessed | tf_op | source)
XLA Modules:
  0.0 103.2 jit_solution(11908778808409858288)
XLA Ops:
  0.6 100.6 %orthogonal.1 = (f32[4096,128]{1,0:T(8,128)S(1)}, f32[4096,128]{1,0:T(8,128)S(1)}) custom-call(f32[4096,128]{1,0:T(8,128)} %bitcast.25, f32[4096,128]{1,0:T(8,128)} %bitcast.26, f32[4096,128]{1,0:T(8,128)} %bitcast.27), custom_call_target="tpu_custom_call" | custom-call | tf_op jit(solution)/shard_map/orthogonal/pallas_call | solution.py:256
  101.2 2.0 %write.1 = (f32[4096,128]{1,0:T(8,128)}, f32[4096,128]{1,0:T(8,128)}) custom-call(f32[4096,128]{1,0:T(8,128)S(1)} %get-tuple-element.6.weights, f32[4096,128]{1,0:T(8,128)S(1)} %get-tuple-element.7.momentum), custom_call_target="tpu_custom_call" | custom-call | tf_op jit(solution)/shard_map/write/pallas_call | solution.py:281
